TPU v7x, 32 devices: a whole 2x2x4 slice. The times are simulated.
32 devices in a mesh: fsdp: 16 (over z, x, core), tp: 2 (over y).
Axes of the slice: x: 2, y: 2, z: 4, core: 2. Of those that a mesh axis runs over, the one named last changes fastest.
Arguments:
- tokens: bfloat16 [2048, 3584], P('fsdp', 'tp'), may hold values from -6 to 6
- norm_gain: bfloat16 [3584], replicated, may hold values from 0.5 to 1.5
- gate_weight: bfloat16 [3584, 10240], P('fsdp', 'tp'), may hold values from -0.09375 to 0.09375
- up_weight: bfloat16 [3584, 10240], P('fsdp', 'tp'), may hold values from -0.09375 to 0.09375
- down_weight: bfloat16 [3584, 10240], P('fsdp', 'tp'), may hold values from -0.0625 to 0.0625
- probes: bfloat16 [2, 3584, 10240], P(None, 'fsdp', 'tp'), may hold values from -0.0625 to 0.0625
Outputs:
- layer_out: bfloat16 [2048, 3584], P('tp', 'fsdp')
- token_curv: float32 [2048], P('tp')
All inputs are finite; a program needn't handle non-finite values.
Results may differ from a plain program's by a relative error of at most 0.014.
Values may be sent and summed in bfloat16 or wider, within the bound.
A program may use at most 128 MiB of HBM per device.

v0:
```python
import jax
import jax.numpy as jnp
from jax import lax
from jax.sharding import PartitionSpec as P

D = 3584
PROBES = 2
epsilon = 1e-06


def on_device(tokens, norm_gain, gate_weight, up_weight, down_weight, probes):
    features = lax.all_gather(tokens, "tp", axis=1, tiled=True)
    widened = features.astype(jnp.float32)
    inverse_rms = lax.rsqrt(jnp.mean(widened * widened, axis=1, keepdims=True) + epsilon)
    normed = (widened * inverse_rms * norm_gain.astype(jnp.float32)).astype(jnp.bfloat16)

    def add_rows(shard_rows):
        return jnp.dot(normed, shard_rows, preferred_element_type=jnp.float32)

    gate_sum = add_rows(lax.all_gather(gate_weight, "fsdp", axis=0, tiled=True))
    up_sum = add_rows(lax.all_gather(up_weight, "fsdp", axis=0, tiled=True))
    hidden = (jax.nn.silu(gate_sum) * up_sum).astype(jnp.bfloat16)
    stacked = jnp.concatenate([down_weight[None], probes], axis=0)
    count = stacked.shape[0]
    col_width = stacked.shape[1]
    flat_weights = stacked.reshape(count * col_width, stacked.shape[2])
    partial_terms = lax.dot_general(
        lax.all_gather(hidden, "fsdp", axis=0, tiled=True),
        flat_weights,
        (((1,), (1,)), ((), ())),
        preferred_element_type=jnp.float32,
    )
    summed = lax.psum_scatter(
        partial_terms.astype(jnp.bfloat16), "tp", scatter_dimension=0, tiled=True
    ).astype(jnp.float32)
    summed_parts = summed.reshape(summed.shape[0], count, col_width)
    primal = summed_parts[:, 0, :]
    tangents = summed_parts[:, 1:, :]
    squashed = jax.nn.sigmoid(primal)
    slope = squashed * (1.0 - squashed)
    tangent_sq = jnp.sum(tangents * tangents, axis=1)
    local_curv = jnp.sum(slope * tangent_sq, axis=1) / (PROBES * D)
    token_curv = lax.psum(local_curv, "fsdp")
    return (primal.astype(jnp.bfloat16), token_curv)


def solution(mesh):
    return jax.shard_map(
        on_device,
        mesh=mesh,
        in_specs=(
            P("fsdp", "tp"),
            P(),
            P("fsdp", "tp"),
            P("fsdp", "tp"),
            P("fsdp", "tp"),
            P(None, "fsdp", "tp"),
        ),
        out_specs=(P("tp", "fsdp"), P("tp")),
        check_vma=False,
    )
```

profile of v0, /device:TPU:0, one launch (start us, length us, event | category | flops | bytes accessed | tf_op | source)
XLA Modules:
  0.0 610.9 jit_solution(12991252066868905236)
XLA Ops:
  7.2 0.0 all-gather.4.cloned.1.call-start
  7.2 0.7 all-gather.4.cloned.1.call-update
  7.9 0.0 all-gather.6.cloned.1.call-start
  8.0 0.7 all-gather.6.cloned.1.call-update
  8.7 0.0 all-gather.8.cloned.1.call-start
  8.7 14.2 %all_gather.12 = bf16[128,3584]{1,0:T(8,128)(2,1)S(1)} all-gather(bf16[128,1792]{1,0:T(8,128)(2,1)S(1)} %copy-done), channel_id=1, replica_groups=mesh['fsdp'=16,'tp'=2] {'tp'}, dimensions={1}, use_global_device_ids=true | all-gather | bytes 1376256 | tf_op jit(solution)/shard_map/all_gather | solution.py:12
  22.9 0.3 fusion.1
  23.2 0.5 add_rsqrt_fusion
  23.7 171.5 %all-gather.4.cloned.1.call-done = bf16[3584,5120]{1,0:T(8,128)(2,1)} async-done(((bf16[224,5120]{1,0:T(8,128)(2,1)}), bf16[3584,5120]{1,0:T(8,128)(2,1)}) %all-gather.4.cloned.1.call-update) | async-done | bytes 36700176 | tf_op jit(solution)/shard_map/all_gather | solution.py:20
  195.2 15.6 %fusion.9 = f32[128,5120]{1,0:T(8,128)S(1)} fusion(bf16[3584,5120]{1,0:T(8,128)(2,1)} %all-gather.4.cloned.1.call-done, bf16[128,3584]{1,0:T(8,128)(2,1)S(1)} %all_gather.12, f32[3584]{0:T(1024)S(1)} %convert_element_type.23, f32[128]{0:T(128)} %add_rsqrt_fusion), kind=kOutput, calls=%fused_computation.16 | convolution fusion | flops 4699455488 | bytes 40253952 | tf_op jit(solution)/shard_map/dot_general | solution.py:18
  210.8 168.9 %all-gather.6.cloned.1.call-done = bf16[3584,5120]{1,0:T(8,128)(2,1)} async-done(((bf16[224,5120]{1,0:T(8,128)(2,1)}), bf16[3584,5120]{1,0:T(8,128)(2,1)}) %all-gather.6.cloned.1.call-update) | async-done | bytes 36700176 | tf_op jit(solution)/shard_map/all_gather | solution.py:21
  379.7 18.0 %fusion = bf16[128,5120]{1,0:T(8,128)(2,1)} fusion(bf16[3584,5120]{1,0:T(8,128)(2,1)} %all-gather.6.cloned.1.call-done, f32[128,5120]{1,0:T(8,128)S(1)} %fusion.9, bf16[128,3584]{1,0:T(8,128)(2,1)S(1)} %all_gather.12, f32[3584]{0:T(1024)S(1)} %convert_element_type.23, f32[128]{0:T(128)} %add_rsqrt_fusion), kind=kOutput, calls=%fused_computation.2 | convolution fusion | flops 4703387648 | bytes 41564672 | tf_op jit(solution)/shard_map/dot_general | solution.py:18
  397.7 0.0 all-gather.8.cloned.1.call-update
  397.7 0.2 reduce-scatter.2.cloned.1.call-start
  397.9 6.5 %pad_maximum_fusion = bf16[3,224,5120]{2,1,0:T(8,128)(2,1)} fusion(bf16[2,224,5120]{2,1,0:T(8,128)(2,1)} %param.11, bf16[1,224,5120]{2,1,0:T(8,128)(2,1)} %bitcast.13), kind=kLoop, calls=%fused_computation | loop fusion | flops 3440640 | bytes 13762560 | tf_op jit(solution)/shard_map/concatenate | solution.py:23
  404.4 102.2 %all-gather.8.cloned.1.call-done = bf16[2048,5120]{1,0:T(8,128)(2,1)} async-done(((bf16[128,5120]{1,0:T(8,128)(2,1)}), bf16[2048,5120]{1,0:T(8,128)(2,1)}) %all-gather.8.cloned.1.call-update) | async-done | bytes 20971536 | tf_op jit(solution)/shard_map/all_gather | solution.py:28
  506.6 21.8 %convolution_convert_fusion = bf16[2048,672]{0,1:T(8,128)(2,1)} fusion(bf16[2048,5120]{1,0:T(8,128)(2,1)} %all-gather.8.cloned.1.call-done, bf16[672,5120]{1,0:T(8,128)(2,1)} %bitcast.12), kind=kOutput, calls=%fused_computation.3 | convolution fusion | flops 14094237696 | bytes 30605312 | tf_op jit(solution)/shard_map/dot_general | solution.py:27
  528.4 0.0 reduce-scatter.2.cloned.1.call-update
  528.4 39.3 %reduce-scatter.2.cloned.1.call-done = bf16[1024,672]{0,1:T(8,128)(2,1)} async-done(((bf16[2048,672]{0,1:T(8,128)(2,1)}), bf16[1024,672]{0,1:T(8,128)(2,1)}) %reduce-scatter.2.cloned.1.call-update) | async-done | bytes 1376272 | tf_op jit(solution)/shard_map/reduce_scatter | solution.py:33
  567.7 1.7 convert.1
  569.4 0.2 fusion.4
  569.6 0.8 fusion.7
  570.5 0.3 fusion.6
  570.8 33.6 %psum.7 = f32[1024]{0:T(1024)} all-reduce(f32[1024]{0:T(1024)S(1)} %broadcast_multiply_fusion), channel_id=1, replica_groups=mesh['fsdp'=16,'tp'=2] {'fsdp'}, use_global_device_ids=true, to_apply=%region_4.5 | all-reduce | flops 1024 | bytes 8192 | tf_op jit(solution)/shard_map/psum | solution.py:43
  (6 shorter events, 0.0 us)
Async XLA Ops:
  7.2 1.6 copy-start.1
  7.2 1.6 copy-start
  7.2 188.0 %all-gather.4.cloned.1.call-start = ((), (), s32[]{:S(2)}) async-start(), calls=%async_computation.1 | async-start | bytes 38993920 | tf_op jit(solution)/shard_map/all_gather | solution.py:20
  7.9 371.8 %all-gather.6.cloned.1.call-start = ((), (), s32[]{:S(2)}) async-start(), calls=%async_computation.2 | async-start | bytes 38993920 | tf_op jit(solution)/shard_map/all_gather | solution.py:21
  8.7 497.9 %all-gather.8.cloned.1.call-start = ((), (), s32[]{:S(2)}) async-start(), calls=%async_computation.3 | async-start | bytes 22282240 | tf_op jit(solution)/shard_map/all_gather | solution.py:28
  397.7 170.0 %reduce-scatter.2.cloned.1.call-start = ((), (), s32[]{:S(2)}) async-start(), calls=%async_computation.4 | async-start | bytes 4128768 | tf_op jit(solution)/shard_map/reduce_scatter | solution.py:33
Sparse Core Ops, SparseCore 0:
  9.6 185.5 all-gather.3
  196.8 182.8 all-gather.5
  397.8 108.7 all-gather.7
  528.6 39.0 reduce-scatter.1
where the time goes:
time: 611 us
  waiting for transfers between devices  483 us (79%)
  matrix products  55.4 us (9%)
  blocking collectives  47.7 us (8%)
  between operations  13.8 us (2%)
  other arithmetic  9.52 us (2%)
    all_gather x1, waiting for transfers between devices, on_device(): gate_sum = add_rows(lax.all_gather(gate_weight, 'fsdp', axis=0, tiled=True))  171 us
    all_gather x1, waiting for transfers between devices, on_device(): up_sum = add_rows(lax.all_gather(up_weight, 'fsdp', axis=0, tiled=True))  169 us
    all_gather x1, waiting for transfers between devices, on_device(): lax.all_gather(hidden, 'fsdp', axis=0, tiled=True)  102 us
    reduce_scatter x1, waiting for transfers between devices, on_device(): lax.psum_scatter(partial_terms.astype(jnp.bfloat16), 'tp', scatter_dimens...  39.3 us
    dot_general x2, matrix products, add_rows(): return jnp.dot(normed, shard_rows, preferred_element_type=jnp.float32)  33.6 us
    psum x1, blocking collectives, on_device(): token_curv = lax.psum(local_curv, 'fsdp')  33.6 us
    dot_general x1, matrix products, on_device(): lax.dot_general(lax.all_gather(hidden, 'fsdp', axis=0, tiled=True), flat_...  21.8 us
    all_gather x1, blocking collectives, on_device(): features = lax.all_gather(tokens, 'tp', axis=1, tiled=True)  14.2 us
  transfers between devices with their start and end apart: 4, of which 4 were waited for; matrix products, arithmetic and copies ran while one was open for 4% of the time, Pallas kernels for 0%

commit v1 on v0

--- a/solution.py
+++ b/solution.py
@@ -40,7 +40,7 @@
     slope = squashed * (1.0 - squashed)
     tangent_sq = jnp.sum(tangents * tangents, axis=1)
     local_curv = jnp.sum(slope * tangent_sq, axis=1) / (PROBES * D)
-    token_curv = lax.psum(local_curv, "fsdp")
+    token_curv = jnp.sum(lax.all_gather(local_curv, "fsdp"), axis=0)
     return (primal.astype(jnp.bfloat16), token_curv)
 
 

time: 611 us -> 600 us (0.982)
  blocking collectives: 47.7 us -> 35.7 us
    psum x1 -> x0, blocking collectives: 33.6 us -> none  [on_device(): token_curv = lax.psum(local_curv, 'fsdp')]
    all_gather x0 -> x1, blocking collectives: none -> 21.5 us  [on_device(): token_curv = jnp.sum(lax.all_gather(local_curv, 'fsdp'), axis=0)]
where the time goes in v1:
time: 600 us; the launch traced here: 599 us
  waiting for transfers between devices  483 us (80%)
  matrix products  55.4 us (9%)
  blocking collectives  35.7 us (6%)
  between operations  13.8 us (2%)
  other arithmetic  10.1 us (2%)
    all_gather x1, waiting for transfers between devices, on_device(): gate_sum = add_rows(lax.all_gather(gate_weight, 'fsdp', axis=0, tiled=True))  171 us
    all_gather x1, waiting for transfers between devices, on_device(): up_sum = add_rows(lax.all_gather(up_weight, 'fsdp', axis=0, tiled=True))  169 us
    all_gather x1, waiting for transfers between devices, on_device(): lax.all_gather(hidden, 'fsdp', axis=0, tiled=True)  102 us
    reduce_scatter x1, waiting for transfers between devices, on_device(): lax.psum_scatter(partial_terms.astype(jnp.bfloat16), 'tp', scatter_dimens...  39.3 us
    dot_general x2, matrix products, add_rows(): return jnp.dot(normed, shard_rows, preferred_element_type=jnp.float32)  33.6 us
    dot_general x1, matrix products, on_device(): lax.dot_general(lax.all_gather(hidden, 'fsdp', axis=0, tiled=True), flat_...  21.8 us
    all_gather x1, blocking collectives, on_device(): token_curv = jnp.sum(lax.all_gather(local_curv, 'fsdp'), axis=0)  21.5 us
    all_gather x1, blocking collectives, on_device(): features = lax.all_gather(tokens, 'tp', axis=1, tiled=True)  14.2 us
  transfers between devices with their start and end apart: 4, of which 4 were waited for; matrix products, arithmetic and copies ran while one was open for 4% of the time, Pallas kernels for 0%

profile of v1, /device:TPU:0, one launch (start us, length us, event | category | flops | bytes accessed | tf_op | source)
XLA Modules:
  0.0 599.4 jit_solution(8364724275810768096)
XLA Ops:
  7.2 0.0 all-gather.5.cloned.1.call-start
  7.2 0.7 all-gather.5.cloned.1.call-update
  7.9 0.0 all-gather.7.cloned.1.call-start
  8.0 0.7 all-gather.7.cloned.1.call-update
  8.7 0.0 all-gather.9.cloned.1.call-start
  8.7 14.2 %all_gather.16 = bf16[128,3584]{1,0:T(8,128)(2,1)S(1)} all-gather(bf16[128,1792]{1,0:T(8,128)(2,1)S(1)} %copy-done), channel_id=1, replica_groups=mesh['fsdp'=16,'tp'=2] {'tp'}, dimensions={1}, use_global_device_ids=true | all-gather | bytes 1376256 | tf_op jit(solution)/shard_map/all_gather | solution.py:12
  22.9 0.3 fusion.1
  23.2 0.5 add_rsqrt_fusion
  23.7 171.5 %all-gather.5.cloned.1.call-done = bf16[3584,5120]{1,0:T(8,128)(2,1)} async-done(((bf16[224,5120]{1,0:T(8,128)(2,1)}), bf16[3584,5120]{1,0:T(8,128)(2,1)}) %all-gather.5.cloned.1.call-update) | async-done | bytes 36700176 | tf_op jit(solution)/shard_map/all_gather | solution.py:20
  195.2 15.6 %fusion.9 = f32[128,5120]{1,0:T(8,128)S(1)} fusion(bf16[3584,5120]{1,0:T(8,128)(2,1)} %all-gather.5.cloned.1.call-done, bf16[128,3584]{1,0:T(8,128)(2,1)S(1)} %all_gather.16, f32[3584]{0:T(1024)S(1)} %convert_element_type.23, f32[128]{0:T(128)} %add_rsqrt_fusion), kind=kOutput, calls=%fused_computation.16 | convolution fusion | flops 4699455488 | bytes 40253952 | tf_op jit(solution)/shard_map/dot_general | solution.py:18
  210.8 168.9 %all-gather.7.cloned.1.call-done = bf16[3584,5120]{1,0:T(8,128)(2,1)} async-done(((bf16[224,5120]{1,0:T(8,128)(2,1)}), bf16[3584,5120]{1,0:T(8,128)(2,1)}) %all-gather.7.cloned.1.call-update) | async-done | bytes 36700176 | tf_op jit(solution)/shard_map/all_gather | solution.py:21
  379.7 18.0 %fusion = bf16[128,5120]{1,0:T(8,128)(2,1)} fusion(bf16[3584,5120]{1,0:T(8,128)(2,1)} %all-gather.7.cloned.1.call-done, f32[128,5120]{1,0:T(8,128)S(1)} %fusion.9, bf16[128,3584]{1,0:T(8,128)(2,1)S(1)} %all_gather.16, f32[3584]{0:T(1024)S(1)} %convert_element_type.23, f32[128]{0:T(128)} %add_rsqrt_fusion), kind=kOutput, calls=%fused_computation.2 | convolution fusion | flops 4703387648 | bytes 41564672 | tf_op jit(solution)/shard_map/dot_general | solution.py:18
  397.7 0.0 all-gather.9.cloned.1.call-update
  397.7 0.2 reduce-scatter.2.cloned.1.call-start
  397.9 6.5 %pad_maximum_fusion = bf16[3,224,5120]{2,1,0:T(8,128)(2,1)} fusion(bf16[2,224,5120]{2,1,0:T(8,128)(2,1)} %param.11, bf16[1,224,5120]{2,1,0:T(8,128)(2,1)} %bitcast.13), kind=kLoop, calls=%fused_computation | loop fusion | flops 3440640 | bytes 13762560 | tf_op jit(solution)/shard_map/concatenate | solution.py:23
  404.4 102.2 %all-gather.9.cloned.1.call-done = bf16[2048,5120]{1,0:T(8,128)(2,1)} async-done(((bf16[128,5120]{1,0:T(8,128)(2,1)}), bf16[2048,5120]{1,0:T(8,128)(2,1)}) %all-gather.9.cloned.1.call-update) | async-done | bytes 20971536 | tf_op jit(solution)/shard_map/all_gather | solution.py:28
  506.6 21.8 %convolution_convert_fusion = bf16[2048,672]{0,1:T(8,128)(2,1)} fusion(bf16[2048,5120]{1,0:T(8,128)(2,1)} %all-gather.9.cloned.1.call-done, bf16[672,5120]{1,0:T(8,128)(2,1)} %bitcast.12), kind=kOutput, calls=%fused_computation.3 | convolution fusion | flops 14094237696 | bytes 30605312 | tf_op jit(solution)/shard_map/dot_general | solution.py:27
  528.4 39.3 %reduce-scatter.2.cloned.1.call-done = bf16[1024,672]{0,1:T(8,128)(2,1)} async-done(((bf16[2048,672]{0,1:T(8,128)(2,1)}), bf16[1024,672]{0,1:T(8,128)(2,1)}) %reduce-scatter.2.cloned.1.call-update) | async-done | bytes 1376272 | tf_op jit(solution)/shard_map/reduce_scatter | solution.py:33
  567.7 1.7 convert.1
  569.4 0.2 fusion.4
  569.6 0.8 fusion.7
  570.5 0.3 fusion.6
  570.8 21.5 %all-gather = f32[16384]{0:T(1024)S(1)} all-gather(f32[1024]{0:T(1024)S(1)} %broadcast_multiply_fusion), channel_id=2, replica_groups=mesh['fsdp'=16,'tp'=2] {'fsdp'}, dimensions={0}, use_global_device_ids=true | all-gather | bytes 69632 | tf_op jit(solution)/shard_map/all_gather | solution.py:43
  592.3 0.6 reduce_sum.39
  (8 shorter events, 0.1 us)
Async XLA Ops:
  7.2 1.6 copy-start.1
  7.2 1.6 copy-start
  7.2 188.0 %all-gather.5.cloned.1.call-start = ((), (), s32[]{:S(2)}) async-start(), calls=%async_computation.1 | async-start | bytes 38993920 | tf_op jit(solution)/shard_map/all_gather | solution.py:20
  7.9 371.8 %all-gather.7.cloned.1.call-start = ((), (), s32[]{:S(2)}) async-start(), calls=%async_computation.2 | async-start | bytes 38993920 | tf_op jit(solution)/shard_map/all_gather | solution.py:21
  8.7 497.9 %all-gather.9.cloned.1.call-start = ((), (), s32[]{:S(2)}) async-start(), calls=%async_computation.3 | async-start | bytes 22282240 | tf_op jit(solution)/shard_map/all_gather | solution.py:28
  397.7 170.0 %reduce-scatter.2.cloned.1.call-start = ((), (), s32[]{:S(2)}) async-start(), calls=%async_computation.4 | async-start | bytes 4128768 | tf_op jit(solution)/shard_map/reduce_scatter | solution.py:33
Sparse Core Ops, SparseCore 0:
  9.6 185.5 all-gather.4
  196.8 182.8 all-gather.6
  397.8 108.7 all-gather.8
  528.6 39.0 reduce-scatter.1
